TPU v7x, 32 devices: a whole 2x2x4 slice. The times are simulated.
32 devices in a mesh: island: 4 (over y, core), shard: 8 (over z, x).
Axes of the slice: x: 2, y: 2, z: 4, core: 2. Of those that a mesh axis runs over, the one named last changes fastest.
Arguments:
- pseudo_grad: float32 [4, 2048, 4096], P('island', 'shard'), may hold values from -6 to 6
- error_buffer: float32 [4, 2048, 4096], P('island', 'shard'), may hold values from -6 to 6
- momentum: float32 [2048, 4096], P('shard'), may hold values from -4 to 4
- weights: bfloat16 [2048, 4096], P('shard'), may hold values from -6 to 6
- warm_basis: float32 [2048, 64], P('shard'), may hold values from -6 to 6
Outputs:
- new_error: float32 [4, 2048, 4096], P('island', 'shard')
- new_momentum: float32 [2048, 4096], P('shard')
- new_weights: bfloat16 [2048, 4096], P('shard')
- new_basis: float32 [2048, 64], P('shard')
All inputs are finite; a program needn't handle non-finite values.
Results may differ from a plain program's by a relative error of at most 0.001.
Values sent between devices are 32-bit elements; how exact they have to be, the bound alone decides.
A program may use at most 128 MiB of HBM per device.

v0:
```python
import jax
import jax.numpy as jnp
from jax import lax
from jax.sharding import PartitionSpec as P

ITERS = 2
HIGH = lax.Precision.HIGHEST
outer_beta = 0.9
outer_rate = 0.7


def orthonormal(factor_rows):
    gram_matrix = jnp.dot(factor_rows, factor_rows.T, precision=HIGH)
    lower_factor = jnp.linalg.cholesky(gram_matrix)
    return lax.linalg.triangular_solve(lower_factor, factor_rows, left_side=True, lower=True)


def on_device(pseudo_grad, error_buffer, momentum, weights, warm_basis):
    merged = (pseudo_grad + error_buffer)[0]
    basis_now = warm_basis
    for iteration in range(ITERS):
        partial_value = lax.dot_general(basis_now, merged, (((0,), (0,)), ((), ())), precision=HIGH)
        factor_rows = orthonormal(lax.psum(partial_value, ("island", "shard")))
        local_proj = lax.dot_general(merged, factor_rows, (((1,), (1,)), ((), ())), precision=HIGH)
        basis_now = lax.psum(local_proj, "island")
    new_error = merged - jnp.dot(local_proj, factor_rows, precision=HIGH)
    update = jnp.dot(basis_now / lax.axis_size("island"), factor_rows, precision=HIGH)
    new_momentum = outer_beta * momentum + update
    stepped = weights.astype(jnp.float32) - outer_rate * (update + outer_beta * new_momentum)
    return (new_error[None], new_momentum, stepped.astype(jnp.bfloat16), basis_now)


def solution(mesh):
    in_specs = (
        P("island", "shard", None),
        P("island", "shard", None),
        P("shard", None),
        P("shard", None),
        P("shard", None),
    )
    out_specs = (P("island", "shard", None), P("shard", None), P("shard", None), P("shard", None))
    return jax.shard_map(
        on_device, mesh=mesh, in_specs=in_specs, out_specs=out_specs, check_vma=False
    )
```

profile of v0, /device:TPU:0, one launch (start us, length us, event | category | flops | bytes accessed | tf_op | source)
XLA Modules:
  0.0 420.1 jit_solution(8857783116008560494)
XLA Ops:
  7.2 0.0 copy-start
  7.2 0.0 all-reduce.5.cloned.1.call-start
  7.2 3.9 add.25
  11.2 0.0 copy-start.1
  11.2 2.0 copy-done.1
  13.2 0.0 copy-done
  13.2 3.8 convolution_bitcast_fusion
  17.0 0.0 all-reduce.5.cloned.1.call-update
  17.0 0.0 all-reduce.7.cloned.1.call-start
  17.1 133.6 %all-reduce.5.cloned.1.call-done = f32[64,4096]{1,0:T(8,128)} async-done(((f32[64,4096]{1,0:T(8,128)}), f32[64,4096]{1,0:T(8,128)}) %all-reduce.5.cloned.1.call-update) | async-done | bytes 1048592 | tf_op jit(solution)/shard_map/psum | solution.py:23
  150.7 2.5 fusion.22
  153.3 0.1 copy.9
  153.3 5.8 %cholesky.44 = f32[64,64]{1,0:T(8,128)S(1)} custom-call(f32[64,64]{1,0:T(8,128)S(1)} %fusion.17), custom_call_target="Cholesky" | custom-call | tf_op jit(solution)/shard_map/jit(cholesky)/cholesky | solution.py:14
  159.2 0.6 compare_reduce_fusion.1
  159.9 0.7 fusion.10
  160.5 4.9 %custom-call.6 = f32[1,64,64]{1,2,0:T(8,128)S(1)} custom-call(f32[1,64,64]{2,1,0:T(8,128)S(1)} %fusion.10), custom_call_target="InvertDiagBlocksLowerTriangular" | custom-call | tf_op jit(solution)/shard_map/triangular_solve/custom-call.0 | solution.py:15
  165.4 2.3 fusion.15
  167.7 5.8 %fusion.5 = f32[256,64]{1,0:T(8,128)} fusion(f32[64,4096]{1,0:T(8,128)S(1)} %fusion.15, f32[1,256,4096]{2,1,0:T(8,128)} %copy-done.1), kind=kOutput, calls=%fused_computation.7 | convolution fusion | flops 805306368 | bytes 5308416 | tf_op jit(solution)/shard_map/dot_general | solution.py:24
  173.5 0.0 all-reduce.7.cloned.1.call-update
  173.6 0.2 all-reduce.9.cloned.1.call-start
  173.8 30.7 %all-reduce.7.cloned.1.call-done = f32[256,64]{1,0:T(8,128)} async-done(((f32[256,64]{1,0:T(8,128)}), f32[256,64]{1,0:T(8,128)}) %all-reduce.7.cloned.1.call-update) | async-done | bytes 65552 | tf_op jit(solution)/shard_map/psum | solution.py:25
  204.4 5.9 %fusion.3 = f32[64,4096]{1,0:T(8,128)} fusion(f32[256,64]{1,0:T(8,128)} %all-reduce.7.cloned.1.call-done, f32[1,256,4096]{2,1,0:T(8,128)} %copy-done.1), kind=kOutput, calls=%fused_computation.5 | convolution fusion | flops 805306368 | bytes 5308416 | tf_op jit(solution)/shard_map/dot_general | solution.py:22
  210.3 0.0 all-reduce.9.cloned.1.call-update
  210.3 130.9 %all-reduce.9.cloned.1.call-done = f32[64,4096]{1,0:T(8,128)} async-done(((f32[64,4096]{1,0:T(8,128)}), f32[64,4096]{1,0:T(8,128)}) %all-reduce.9.cloned.1.call-update) | async-done | bytes 1048592 | tf_op jit(solution)/shard_map/psum | solution.py:23
  341.2 2.5 fusion.23
  343.8 0.1 copy.10
  343.9 5.8 %cholesky.55 = f32[64,64]{1,0:T(8,128)S(1)} custom-call(f32[64,64]{1,0:T(8,128)S(1)} %fusion.14), custom_call_target="Cholesky" | custom-call | tf_op jit(solution)/shard_map/jit(cholesky)/cholesky | solution.py:14
  349.7 0.6 compare_reduce_fusion
  350.4 0.7 fusion.11
  351.1 4.9 %custom-call.7 = f32[1,64,64]{1,2,0:T(8,128)S(1)} custom-call(f32[1,64,64]{2,1,0:T(8,128)S(1)} %fusion.11), custom_call_target="InvertDiagBlocksLowerTriangular" | custom-call | tf_op jit(solution)/shard_map/triangular_solve/custom-call.0 | solution.py:15
  355.9 2.3 fusion.12
  358.2 6.1 %fusion.1 = f32[256,64]{0,1:T(8,128)S(1)} fusion(f32[64,4096]{1,0:T(8,128)S(1)} %fusion.12, f32[1,256,4096]{2,1,0:T(8,128)} %copy-done.1), kind=kOutput, calls=%fused_computation.3 | convolution fusion | flops 805306368 | bytes 5308416 | tf_op jit(solution)/shard_map/dot_general | solution.py:24
  364.3 0.0 copy-start.3
  364.3 0.0 copy-start.2
  364.4 6.8 %fusion = f32[1,256,4096]{2,1,0:T(8,128)} fusion(f32[256,64]{0,1:T(8,128)S(1)} %fusion.1, f32[64,4096]{1,0:T(8,128)S(1)} %fusion.12, f32[1,256,4096]{2,1,0:T(8,128)} %copy-done.1), kind=kOutput, calls=%fused_computation.1 | convolution fusion | flops 806354944 | bytes 9502720 | tf_op jit(solution)/shard_map/dot_general | solution.py:26
  371.1 0.0 copy-done.3
  371.1 0.0 all-reduce.11.cloned.1.call-start
  371.1 0.6 all-reduce.11.cloned.1.call-update
  371.7 33.3 %all-reduce.11.cloned.1.call-done = f32[256,64]{0,1:T(8,128)} async-done(((f32[256,64]{0,1:T(8,128)}), f32[256,64]{0,1:T(8,128)}) %all-reduce.11.cloned.1.call-update) | async-done | bytes 65552 | tf_op jit(solution)/shard_map/psum | solution.py:25
  405.0 0.0 copy-done.2
  405.0 0.0 copy-start.4
  405.0 7.9 %subtract_convert_fusion = (bf16[256,4096]{1,0:T(8,128)(2,1)}, f32[256,4096]{1,0:T(8,128)}) fusion(bf16[256,4096]{1,0:T(8,128)(2,1)S(1)} %copy-done.2, f32[256,4096]{1,0:T(8,128)} %param.10, f32[64,4096]{1,0:T(8,128)S(1)} %fusion.12, f32[256,64]{0,1:T(8,128)} %all-reduce.11.cloned.1.call-done), kind=kOutput, calls=%fused_computation.10 | convolution fusion | flops 813711360 | bytes 13697024 | tf_op jit(solution)/shard_map/dot_general | solution.py:27
  412.9 0.0 copy-done.4
  412.9 0.6 copy.15
  (4 shorter events, 0.1 us)
Async XLA Ops:
  7.2 6.0 %copy-start = (f32[256,64]{0,1:T(8,128)S(1)}, f32[256,64]{0,1:T(8,128)}, u32[]{:S(2)}) copy-start(f32[256,64]{0,1:T(8,128)} %param.12) | copy-start | bytes 196612
  7.2 143.5 %all-reduce.5.cloned.1.call-start = ((), (), s32[]{:S(2)}) async-start(), calls=%async_computation | async-start | bytes 2097152 | tf_op jit(solution)/shard_map/psum | solution.py:23
  11.2 2.0 copy-start.1
  17.0 187.4 %all-reduce.7.cloned.1.call-start = ((), (), s32[]{:S(2)}) async-start(), calls=%async_computation.1 | async-start | bytes 262144 | tf_op jit(solution)/shard_map/psum | solution.py:25
  173.6 167.7 %all-reduce.9.cloned.1.call-start = ((), (), s32[]{:S(2)}) async-start(), calls=%async_computation.2 | async-start | bytes 2097152 | tf_op jit(solution)/shard_map/psum | solution.py:23
  364.3 6.8 %copy-start.3 = (f32[256,64]{0,1:T(8,128)}, f32[256,64]{0,1:T(8,128)S(1)}, u32[]{:S(2)}) copy-start(f32[256,64]{0,1:T(8,128)S(1)} %fusion.1) | copy-start | bytes 196612
  364.3 40.7 %copy-start.2 = (bf16[256,4096]{1,0:T(8,128)(2,1)S(1)}, bf16[256,4096]{1,0:T(8,128)(2,1)}, u32[]{:S(2)}) copy-start(bf16[256,4096]{1,0:T(8,128)(2,1)} %param.11) | copy-start | bytes 6291460
  371.1 33.9 %all-reduce.11.cloned.1.call-start = ((), (), s32[]{:S(2)}) async-start(), calls=%async_computation.3 | async-start | bytes 131072 | tf_op jit(solution)/shard_map/psum | solution.py:25
  405.0 7.9 %copy-start.4 = (f32[256,64]{0,1:T(8,128)S(1)}, f32[256,64]{0,1:T(8,128)}, u32[]{:S(2)}) copy-start(f32[256,64]{0,1:T(8,128)} %all-reduce.11.cloned.1.call-done) | copy-start | bytes 196612
Sparse Core Ops, SparseCore 0:
  17.2 133.5 all-reduce.4
  173.7 30.7 all-reduce.6
  210.5 130.7 all-reduce.8
  374.5 30.4 all-reduce.10
where the time goes:
time: 420 us
  waiting for transfers between devices  329 us (78%)
  matrix products  45.8 us (11%)
  other arithmetic  28.1 us (7%)
  between operations  13.9 us (3%)
    psum x2, waiting for transfers between devices, on_device(): factor_rows = orthonormal(lax.psum(partial_value, ('island', 'shard')))  265 us
    psum x2, waiting for transfers between devices, on_device(): basis_now = lax.psum(local_proj, 'island')  64 us
    another operation x6, other arithmetic, orthonormal(): lower_factor = jnp.linalg.cholesky(gram_matrix)  13 us
    dot_general x2, matrix products, on_device(): lax.dot_general(merged, factor_rows, (((1,), (1,)), ((), ())), precision=...  11.9 us
    another operation x4, other arithmetic, orthonormal(): lax.linalg.triangular_solve(lower_factor, factor_rows, left_side=True, lo...  11.1 us
    dot_general x2, matrix products, on_device(): lax.dot_general(basis_now, merged, (((0,), (0,)), ((), ())), precision=HIGH)  9.69 us
  transfers between devices with their start and end apart: 4, of which 4 were waited for; matrix products, arithmetic and copies ran while one was open for 0% of the time, Pallas kernels for 0%

commit v1 on v0

--- a/solution.py
+++ b/solution.py
@@ -22,7 +22,7 @@
         partial_value = lax.dot_general(basis_now, merged, (((0,), (0,)), ((), ())), precision=HIGH)
         factor_rows = orthonormal(lax.psum(partial_value, ("island", "shard")))
         local_proj = lax.dot_general(merged, factor_rows, (((1,), (1,)), ((), ())), precision=HIGH)
-        basis_now = lax.psum(local_proj, "island")
+        basis_now = jnp.sum(lax.all_gather(local_proj, "island"), axis=0)
     new_error = merged - jnp.dot(local_proj, factor_rows, precision=HIGH)
     update = jnp.dot(basis_now / lax.axis_size("island"), factor_rows, precision=HIGH)
     new_momentum = outer_beta * momentum + update

time: 420 us -> 367 us (0.87)
  waiting for transfers between devices: 329 us -> 264 us
  blocking collectives: 0 us -> 12.4 us
    psum x2 -> x0, waiting for transfers between devices: 64 us -> none  [on_device(): basis_now = lax.psum(local_proj, 'island')]
    all_gather x0 -> x2, blocking collectives: none -> 12.4 us  [on_device(): basis_now = jnp.sum(lax.all_gather(local_proj, 'island'), axis=0)]
  transfers between devices with their start and end apart: 4 -> 2, of which waited for: 4 -> 2; matrix products, arithmetic and copies ran while one was open for 0% -> 0% of each run, Pallas kernels for 0% -> 0%
where the time goes in v1:
time: 367 us
  waiting for transfers between devices  264 us (72%)
  matrix products  44.5 us (12%)
  other arithmetic  28.4 us (8%)
  between operations  14.2 us (4%)
  blocking collectives  12.4 us (3%)
    psum x2, waiting for transfers between devices, on_device(): factor_rows = orthonormal(lax.psum(partial_value, ('island', 'shard')))  264 us
    another operation x6, other arithmetic, orthonormal(): lower_factor = jnp.linalg.cholesky(gram_matrix)  13 us
    all_gather x2, blocking collectives, on_device(): basis_now = jnp.sum(lax.all_gather(local_proj, 'island'), axis=0)  12.4 us
    dot_general x2, matrix products, on_device(): lax.dot_general(merged, factor_rows, (((1,), (1,)), ((), ())), precision=...  12.2 us
    another operation x4, other arithmetic, orthonormal(): lax.linalg.triangular_solve(lower_factor, factor_rows, left_side=True, lo...  11.1 us
    dot_general x2, matrix products, on_device(): lax.dot_general(basis_now, merged, (((0,), (0,)), ((), ())), precision=HIGH)  9.6 us
    dot_general x1, matrix products, on_device(): jnp.dot(basis_now / lax.axis_size('island'), factor_rows, precision=HIGH)  7.85 us
  transfers between devices with their start and end apart: 2, of which 2 were waited for; matrix products, arithmetic and copies ran while one was open for 0% of the time, Pallas kernels for 0%

profile of v1, /device:TPU:0, one launch (start us, length us, event | category | flops | bytes accessed | tf_op | source)
XLA Modules:
  0.0 366.5 jit_solution(98535912545339685)
XLA Ops:
  7.2 0.0 copy-start
  7.2 0.0 all-reduce.3.cloned.1.call-start
  7.2 3.9 %add.21 = f32[1,256,4096]{2,1,0:T(8,128)S(1)} add(f32[1,256,4096]{2,1,0:T(8,128)} %param.8, f32[1,256,4096]{2,1,0:T(8,128)} %param.9) | non-fusion elementwise | flops 1048576 | bytes 12582912 | tf_op jit(solution)/shard_map/add | solution.py:19
  11.2 0.0 copy-start.1
  11.2 2.0 copy-done.1
  13.2 0.0 copy-done
  13.2 3.8 %convolution_bitcast_fusion = f32[64,4096]{1,0:T(8,128)} fusion(f32[256,64]{0,1:T(8,128)S(1)} %copy-done, f32[1,256,4096]{2,1,0:T(8,128)S(1)} %add.21), kind=kOutput, calls=%fused_computation.2 | convolution fusion | flops 805306368 | bytes 5308416 | tf_op jit(solution)/shard_map/dot_general | solution.py:22
  17.0 0.0 all-reduce.3.cloned.1.call-update
  17.0 0.0 all-reduce.5.cloned.1.call-start
  17.1 133.6 %all-reduce.3.cloned.1.call-done = f32[64,4096]{1,0:T(8,128)} async-done(((f32[64,4096]{1,0:T(8,128)}), f32[64,4096]{1,0:T(8,128)}) %all-reduce.3.cloned.1.call-update) | async-done | bytes 1048592 | tf_op jit(solution)/shard_map/psum | solution.py:23
  150.7 2.5 fusion.22
  153.3 0.1 copy.11
  153.3 5.8 %cholesky.44 = f32[64,64]{1,0:T(8,128)S(1)} custom-call(f32[64,64]{1,0:T(8,128)S(1)} %fusion.17), custom_call_target="Cholesky" | custom-call | tf_op jit(solution)/shard_map/jit(cholesky)/cholesky | solution.py:14
  159.2 0.6 compare_reduce_fusion.1
  159.9 0.7 fusion.10
  160.5 4.9 %custom-call.6 = f32[1,64,64]{1,2,0:T(8,128)S(1)} custom-call(f32[1,64,64]{2,1,0:T(8,128)S(1)} %fusion.10), custom_call_target="InvertDiagBlocksLowerTriangular" | custom-call | tf_op jit(solution)/shard_map/triangular_solve/custom-call.0 | solution.py:15
  165.4 2.3 fusion.15
  167.7 6.1 %fusion.5 = f32[256,64]{0,1:T(8,128)S(1)} fusion(f32[64,4096]{1,0:T(8,128)S(1)} %fusion.15, f32[1,256,4096]{2,1,0:T(8,128)} %copy-done.1), kind=kOutput, calls=%fused_computation.7 | convolution fusion | flops 805306368 | bytes 5308416 | tf_op jit(solution)/shard_map/dot_general | solution.py:24
  173.8 6.0 %all-gather = f32[1024,64]{0,1:T(8,128)S(1)} all-gather(f32[256,64]{0,1:T(8,128)S(1)} %fusion.5), channel_id=2, replica_groups=mesh['island'=4,'shard'=8] {'island'}, dimensions={0}, use_global_device_ids=true | all-gather | bytes 327680 | tf_op jit(solution)/shard_map/all_gather | solution.py:25
  179.8 0.1 reshape.21
  179.9 0.2 reduce_sum.18
  180.1 5.8 %fusion.3 = f32[64,4096]{1,0:T(8,128)} fusion(f32[256,64]{0,1:T(8,128)S(1)} %reduce_sum.18, f32[1,256,4096]{2,1,0:T(8,128)} %copy-done.1), kind=kOutput, calls=%fused_computation.5 | convolution fusion | flops 805306368 | bytes 5308416 | tf_op jit(solution)/shard_map/dot_general | solution.py:22
  185.9 0.0 all-reduce.5.cloned.1.call-update
  185.9 129.9 %all-reduce.5.cloned.1.call-done = f32[64,4096]{1,0:T(8,128)} async-done(((f32[64,4096]{1,0:T(8,128)}), f32[64,4096]{1,0:T(8,128)}) %all-reduce.5.cloned.1.call-update) | async-done | bytes 1048592 | tf_op jit(solution)/shard_map/psum | solution.py:23
  315.8 2.5 fusion.23
  318.3 0.1 copy.12
  318.4 5.8 %cholesky.55 = f32[64,64]{1,0:T(8,128)S(1)} custom-call(f32[64,64]{1,0:T(8,128)S(1)} %fusion.14), custom_call_target="Cholesky" | custom-call | tf_op jit(solution)/shard_map/jit(cholesky)/cholesky | solution.py:14
  324.3 0.6 compare_reduce_fusion
  324.9 0.7 fusion.11
  325.6 4.9 %custom-call.7 = f32[1,64,64]{1,2,0:T(8,128)S(1)} custom-call(f32[1,64,64]{2,1,0:T(8,128)S(1)} %fusion.11), custom_call_target="InvertDiagBlocksLowerTriangular" | custom-call | tf_op jit(solution)/shard_map/triangular_solve/custom-call.0 | solution.py:15
  330.5 0.0 copy-start.2
  330.5 2.4 fusion.12
  332.9 6.1 %fusion.1 = f32[256,64]{0,1:T(8,128)S(1)} fusion(f32[64,4096]{1,0:T(8,128)S(1)} %fusion.12, f32[1,256,4096]{2,1,0:T(8,128)} %copy-done.1), kind=kOutput, calls=%fused_computation.3 | convolution fusion | flops 805306368 | bytes 5308416 | tf_op jit(solution)/shard_map/dot_general | solution.py:24
  339.0 0.0 copy-done.2
  339.0 0.0 copy-start.3
  339.0 5.1 %fusion = f32[1,256,4096]{2,1,0:T(8,128)} fusion(f32[256,64]{0,1:T(8,128)S(1)} %fusion.1, f32[64,4096]{1,0:T(8,128)S(1)} %fusion.12, f32[1,256,4096]{2,1,0:T(8,128)S(1)} %copy-done.2), kind=kOutput, calls=%fused_computation.1 | convolution fusion | flops 806354944 | bytes 9502720 | tf_op jit(solution)/shard_map/dot_general | solution.py:26
  344.2 6.4 %all-gather.1 = f32[1024,64]{0,1:T(8,128)} all-gather(f32[256,64]{0,1:T(8,128)S(1)} %fusion.1), channel_id=3, replica_groups=mesh['island'=4,'shard'=8] {'island'}, dimensions={0}, use_global_device_ids=true | all-gather | bytes 327680 | tf_op jit(solution)/shard_map/all_gather | solution.py:25
  350.6 1.1 reshape.22
  351.7 0.2 reduce_sum.19
  351.8 0.0 copy-done.3
  351.8 0.0 copy-start.4
  351.8 7.8 %subtract_convert_fusion = (bf16[256,4096]{1,0:T(8,128)(2,1)}, f32[256,4096]{1,0:T(8,128)}) fusion(bf16[256,4096]{1,0:T(8,128)(2,1)S(1)} %copy-done.3, f32[256,4096]{1,0:T(8,128)} %param.10, f32[64,4096]{1,0:T(8,128)S(1)} %fusion.12, f32[256,64]{0,1:T(8,128)S(1)} %reduce_sum.19), kind=kOutput, calls=%fused_computation.10 | convolution fusion | flops 813711360 | bytes 13697024 | tf_op jit(solution)/shard_map/dot_general | solution.py:27
  359.7 0.0 copy-done.4
  (4 shorter events, 0.1 us)
Async XLA Ops:
  7.2 6.0 %copy-start = (f32[256,64]{0,1:T(8,128)S(1)}, f32[256,64]{0,1:T(8,128)}, u32[]{:S(2)}) copy-start(f32[256,64]{0,1:T(8,128)} %param.12) | copy-start | bytes 196612
  7.2 143.5 %all-reduce.3.cloned.1.call-start = ((), (), s32[]{:S(2)}) async-start(), calls=%async_computation | async-start | bytes 2097152 | tf_op jit(solution)/shard_map/psum | solution.py:23
  11.2 2.0 copy-start.1
  17.0 298.7 %all-reduce.5.cloned.1.call-start = ((), (), s32[]{:S(2)}) async-start(), calls=%async_computation.1 | async-start | bytes 2097152 | tf_op jit(solution)/shard_map/psum | solution.py:23
  330.5 8.5 %copy-start.2 = (f32[1,256,4096]{2,1,0:T(8,128)S(1)}, f32[1,256,4096]{2,1,0:T(8,128)}, u32[]{:S(2)}) copy-start(f32[1,256,4096]{2,1,0:T(8,128)} %copy-done.1) | copy-start | bytes 12582916
  339.0 12.8 %copy-start.3 = (bf16[256,4096]{1,0:T(8,128)(2,1)S(1)}, bf16[256,4096]{1,0:T(8,128)(2,1)}, u32[]{:S(2)}) copy-start(bf16[256,4096]{1,0:T(8,128)(2,1)} %param.11) | copy-start | bytes 6291460
  351.8 7.9 %copy-start.4 = (f32[256,64]{0,1:T(8,128)}, f32[256,64]{0,1:T(8,128)S(1)}, u32[]{:S(2)}) copy-start(f32[256,64]{0,1:T(8,128)S(1)} %reduce_sum.19) | copy-start | bytes 196612
Sparse Core Ops, SparseCore 0:
  17.2 133.5 all-reduce.2
  186.0 129.7 all-reduce.4
